TPU v7x, 32 devices: a whole 2x2x4 slice. The times are simulated.
32 devices in a mesh: wide: 8 (over y, x, core), pair: 4 (over z).
Axes of the slice: x: 2, y: 2, z: 4, core: 2. Of those that a mesh axis runs over, the one named last changes fastest.
Arguments:
- rhs: bfloat16 [32768, 512], P(('wide', 'pair')), may hold values from -6 to 6
- coords: bfloat16 [64, 2, 512], P(('wide', 'pair')), may hold values from 0 to 1
- near_index: int32 [64, 3], P(('wide', 'pair')), may hold values from -2 to 2, as said below
- project_basis: bfloat16 [64, 512, 192], P(('wide', 'pair')), may hold values from -0.25 to 0.25
- expand_basis: bfloat16 [64, 512, 192], P(('wide', 'pair')), may hold values from -0.4375 to 0.4375
- transfer: bfloat16 [32, 5, 2, 192, 192], P(('wide', 'pair')), may hold values from -0.3125 to 0.3125
- level_perm: int32 [5, 192], replicated, may hold values from 0 to 191, each once within a row
Outputs:
- applied: bfloat16 [32768, 512], P(('wide', 'pair'))
Inputs may be any that keep to these rules, and one draw needn't show every extreme that they name: `near_index`: each row holds 3 different offsets. `level_perm`: each row is a permutation of 0 to 191.
All inputs are finite; a program needn't handle non-finite values.
Results may differ from a plain program's by a relative error of at most 0.0095.
Values may be sent and summed in bfloat16 or wider, within the bound.
A program may use at most 64 MiB of HBM per device.

v0:
```python
import math

import jax
import jax.numpy as jnp
from jax import lax
from jax.sharding import PartitionSpec as P

NB = 3
LW = 3
LP = 2


softening = 0.0004


def padded(x, sides, width):
    for axis, dim in sides:
        devices, length = (lax.axis_size(axis), x.shape[dim])
        up = [(i, (i + 1) % devices) for i in range(devices - 1)]
        down = [(j, i) for i, j in up]
        last = lax.slice_in_dim(x, length - width, length, axis=dim)
        initial = lax.slice_in_dim(x, 0, width, axis=dim)
        before = lax.ppermute(last, axis, up)
        after = lax.ppermute(initial, axis, down)
        x = jnp.concatenate([before, x, after], axis=dim)
    return x


def from_partner(block, axis, bit):
    count = lax.axis_size(axis)
    route = []
    for low in range(count):
        high = low | 1 << bit
        if high != low and high < count:
            route += [(low, high), (high, low)]
    return lax.ppermute(block, axis, route)


def kernel_tile(target, source):
    delta_x = target[0][:, None] - source[0][None, :]
    delta_y = target[1][:, None] - source[1][None, :]
    factor = 0.25 / math.sqrt(target.shape[1])
    return (lax.rsqrt(delta_x * delta_x + delta_y * delta_y + softening) * factor).astype(
        jnp.bfloat16
    )


def on_device(rhs, coords, near_index, project_basis, expand_basis, transfer, level_perm):
    own_leaves = coords.shape[0]
    leaf_rows = coords.shape[2]
    columns = rhs.shape[1]
    leaves = rhs.reshape(own_leaves, leaf_rows, columns)
    points = coords.astype(jnp.float32)
    padded_rhs, padded_points = (
        padded(leaves, ((("wide", "pair"), 0),), 2),
        padded(coords, ((("wide", "pair"), 0),), 2),
    )
    gathered = []
    for target in range(own_leaves):
        summed = jnp.zeros((leaf_rows, columns), jnp.float32)
        for slot in range(NB):
            position = target + 2 + near_index[target, slot]
            source_rows = lax.dynamic_index_in_dim(padded_rhs, position, 0, keepdims=False)
            source_points = lax.dynamic_index_in_dim(
                padded_points, position, 0, keepdims=False
            ).astype(jnp.float32)
            tile = kernel_tile(points[target], source_points)
            summed = summed + jnp.dot(tile, source_rows, preferred_element_type=jnp.float32)
        gathered.append(summed)
    nearby = jnp.stack(gathered)
    projected = jnp.zeros((project_basis.shape[2], columns), jnp.float32)
    for target in range(own_leaves):
        projected = projected + jnp.einsum(
            "lr,lc->rc", project_basis[target], leaves[target], preferred_element_type=jnp.float32
        )
    projected = projected.astype(jnp.bfloat16)
    for level_bit in range(LW):
        partner_rows = from_partner(projected, "wide", level_bit)[level_perm[level_bit]]
        updated = jnp.dot(transfer[0, level_bit, 0], projected, preferred_element_type=jnp.float32)
        updated = updated + jnp.dot(
            transfer[0, level_bit, 1], partner_rows, preferred_element_type=jnp.float32
        )
        projected = updated.astype(jnp.bfloat16)
    for level_bit in range(LP):
        partner_rows = from_partner(projected, "pair", level_bit)[level_perm[LW + level_bit]]
        updated = jnp.dot(
            transfer[0, LW + level_bit, 0], projected, preferred_element_type=jnp.float32
        )
        updated = updated + jnp.dot(
            transfer[0, LW + level_bit, 1], partner_rows, preferred_element_type=jnp.float32
        )
        projected = updated.astype(jnp.bfloat16)
    distant = jnp.einsum("nlr,rc->nlc", expand_basis, projected, preferred_element_type=jnp.float32)
    return (nearby + distant).reshape(own_leaves * leaf_rows, columns).astype(jnp.bfloat16)


def solution(mesh):
    return jax.shard_map(
        on_device,
        mesh=mesh,
        in_specs=(
            P(("wide", "pair"), None),
            P(("wide", "pair"), None, None),
            P(("wide", "pair"), None),
            P(("wide", "pair"), None, None),
            P(("wide", "pair"), None, None),
            P(("wide", "pair"), None, None, None, None),
            P(),
        ),
        out_specs=P(("wide", "pair"), None),
        check_vma=False,
    )
```

profile of v0, /device:TPU:1, one launch (start us, length us, event | category | flops | bytes accessed | tf_op | source)
XLA Modules:
  0.0 85.5 jit_solution(957813093122317052)
XLA Ops:
  0.0 4.1 %collective-permute-start = (bf16[2,2,512]{2,1,0:T(2,128)(2,1)}, bf16[2,2,512]{2,1,0:T(2,128)(2,1)S(1)}, u32[]{:S(2)}, u32[]{:S(2)}) collective-permute-start(bf16[2,2,512]{2,1,0:T(2,128)(2,1)} %param.8), channel_id=1, source_target_pairs={{0,1},{1,2},{2,3},{3,4},{4,5},{5,6},{6,7},{7,8},{8,9},{9,10},{10,1... | collective-permute-start | bytes 12296 | tf_op jit(solution)/shard_map/ppermute | solution.py:23
  4.2 4.5 %collective-permute-start.1 = (bf16[2,2,512]{2,1,0:T(2,128)(2,1)}, bf16[2,2,512]{2,1,0:T(2,128)(2,1)S(1)}, u32[]{:S(2)}, u32[]{:S(2)}) collective-permute-start(bf16[2,2,512]{2,1,0:T(2,128)(2,1)} %param.8), channel_id=1, source_target_pairs={{1,0},{2,1},{3,2},{4,3},{5,4},{6,5},{7,6},{8,7},{9,8},{10,9},{11,1... | collective-permute-start | bytes 12296 | tf_op jit(solution)/shard_map/ppermute | solution.py:24
  8.7 1.9 %collective-permute-start.2 = (bf16[2,512,512]{2,1,0:T(8,128)(2,1)}, bf16[2,512,512]{2,1,0:T(8,128)(2,1)S(1)}, u32[]{:S(2)}, u32[]{:S(2)}) collective-permute-start(bf16[2,512,512]{2,1,0:T(8,128)(2,1)} %bitcast.125), channel_id=1, source_target_pairs={{0,1},{1,2},{2,3},{3,4},{4,5},{5,6},{6,7},{7,8},{8,9},{9,10},{10,1... | collective-permute-start | bytes 3145736 | tf_op jit(solution)/shard_map/ppermute | solution.py:23
  10.6 5.4 %collective-permute-start.3 = (bf16[2,512,512]{2,1,0:T(8,128)(2,1)}, bf16[2,512,512]{2,1,0:T(8,128)(2,1)}, u32[]{:S(2)}, u32[]{:S(2)}) collective-permute-start(bf16[2,512,512]{2,1,0:T(8,128)(2,1)} %bitcast.126), channel_id=1, source_target_pairs={{1,0},{2,1},{3,2},{4,3},{5,4},{6,5},{7,6},{8,7},{9,8},{10,9},{11,1... | collective-permute-start | bytes 3145736 | tf_op jit(solution)/shard_map/ppermute | solution.py:24
  16.1 1.4 %fusion.23 = f32[192,512]{1,0:T(8,128)S(1)} fusion(bf16[1024,512]{1,0:T(8,128)(2,1)} %param.7, bf16[2,512,192]{1,2,0:T(8,128)(2,1)} %param.10), kind=kOutput, calls=%fused_computation.44 | convolution fusion | flops 100663296 | bytes 1114112 | tf_op jit(solution)/shard_map/lr,lc->rc/dot_general | solution.py:73
  17.5 1.4 %fusion.10 = bf16[192,512]{1,0:T(8,128)(2,1)S(1)} fusion(f32[192,512]{1,0:T(8,128)S(1)} %fusion.23, bf16[1024,512]{1,0:T(8,128)(2,1)} %param.7, bf16[2,512,192]{1,2,0:T(8,128)(2,1)} %param.10), kind=kOutput, calls=%fused_computation.25 | convolution fusion | flops 100859904 | bytes 1310720 | tf_op jit(solution)/shard_map/lr,lc->rc/dot_general | solution.py:73
  19.0 0.8 fusion.124
  19.7 1.6 %fusion.129 = (s32[1,1]{1,0:T(1,128)}, s32[1,1]{1,0:T(1,128)}, s32[1,1]{1,0:T(1,128)}, s32[1,1]{1,0:T(1,128)}, s32[1,1]{1,0:T(1,128)}, /*index=5*/s32[1,1]{1,0:T(1,128)}) fusion(s32[2,3]{1,0:T(2,128)} %param.9), kind=kLoop, calls=%fused_computation.167 | loop fusion | bytes 48 | tf_op jit(solution)/shard_map/slice | solution.py:62
  21.3 0.9 %compare_select_fusion = (s32[192,1]{0,1:T(1,128)S(1)}, s32[192,1]{0,1:T(1,128)S(1)}, s32[192,1]{0,1:T(1,128)S(1)}, s32[192,1]{0,1:T(1,128)S(1)}, s32[192,1]{0,1:T(1,128)S(1)}) fusion(s32[5,192]{1,0:T(8,128)} %param.13), kind=kLoop, calls=%fused_computation.120 | loop fusion | flops 2880 | bytes 7680 | tf_op jit(solution)/shard_map/select_n | solution.py:85
  22.2 1.1 %fusion.85 = f32[512,192]{0,1:T(8,128)S(1)} fusion(bf16[192,512]{1,0:T(8,128)(2,1)S(1)} %fusion.10, bf16[1,5,2,192,192]{4,3,2,1,0:T(8,128)(2,1)} %param.12), kind=kOutput, calls=%fused_computation.105 | convolution fusion | flops 37748736 | bytes 688128 | tf_op jit(solution)/shard_map/dot_general | solution.py:79
  31.0 1.0 %gather_fusion = bf16[192,512]{1,0:T(8,128)(2,1)S(1)} fusion(bf16[192,512]{1,0:T(8,128)(2,1)S(1)} %collective-permute-done.4, s32[1024]{0:T(1024)S(1)} %pad_clamp_fusion.4), kind=kCustom, calls=%fused_computation | custom fusion | bytes 393984 | tf_op jit(solution)/shard_map/gather | solution.py:78
  32.0 1.1 %fusion.5 = bf16[512,192]{0,1:T(8,128)(2,1)S(1)} fusion(f32[512,192]{0,1:T(8,128)S(1)} %fusion.85, bf16[192,512]{1,0:T(8,128)(2,1)S(1)} %gather_fusion, bf16[1,5,2,192,192]{4,3,2,1,0:T(8,128)(2,1)} %param.12), kind=kOutput, calls=%fused_computation.20 | convolution fusion | flops 37945344 | bytes 884736 | tf_op jit(solution)/shard_map/dot_general | solution.py:80
  33.1 3.4 %collective-permute-start.5 = (bf16[192,512]{1,0:T(8,128)(2,1)S(1)}, bf16[192,512]{1,0:T(8,128)(2,1)S(1)}, u32[]{:S(2)}, u32[]{:S(2)}) collective-permute-start(bf16[192,512]{1,0:T(8,128)(2,1)S(1)} %bitcast.128), channel_id=1, source_target_pairs={{0,8},{8,0},{4,12},{12,4},{16,24},{24,16},{20,28},{28,20},{1,9},{9... | collective-permute-start | bytes 589832 | tf_op jit(solution)/shard_map/ppermute | solution.py:36
  36.5 1.1 %fusion.82 = f32[512,192]{0,1:T(8,128)S(1)} fusion(bf16[512,192]{0,1:T(8,128)(2,1)S(1)} %fusion.5, bf16[1,5,2,192,192]{4,3,2,1,0:T(8,128)(2,1)} %param.12), kind=kOutput, calls=%fused_computation.102 | convolution fusion | flops 37748736 | bytes 688128 | tf_op jit(solution)/shard_map/dot_general | solution.py:79
  37.6 6.3 %collective-permute-done.5 = bf16[192,512]{1,0:T(8,128)(2,1)S(1)} collective-permute-done((bf16[192,512]{1,0:T(8,128)(2,1)S(1)}, bf16[192,512]{1,0:T(8,128)(2,1)S(1)}, u32[]{:S(2)}, u32[]{:S(2)}) %collective-permute-start.5) | collective-permute-done | bytes 196640 | tf_op jit(solution)/shard_map/ppermute | solution.py:36
  43.9 1.0 %gather_fusion.1 = bf16[192,512]{1,0:T(8,128)(2,1)S(1)} fusion(bf16[192,512]{1,0:T(8,128)(2,1)S(1)} %collective-permute-done.5, s32[1024]{0:T(1024)S(1)} %pad_clamp_fusion.3), kind=kCustom, calls=%fused_computation.1 | custom fusion | bytes 393984 | tf_op jit(solution)/shard_map/gather | solution.py:78
  44.9 1.1 %fusion.6 = bf16[512,192]{0,1:T(8,128)(2,1)S(1)} fusion(f32[512,192]{0,1:T(8,128)S(1)} %fusion.82, bf16[192,512]{1,0:T(8,128)(2,1)S(1)} %gather_fusion.1, bf16[1,5,2,192,192]{4,3,2,1,0:T(8,128)(2,1)} %param.12), kind=kOutput, calls=%fused_computation.21 | convolution fusion | flops 37945344 | bytes 884736 | tf_op jit(solution)/shard_map/dot_general | solution.py:80
  46.0 1.0 %collective-permute-start.6 = (bf16[192,512]{1,0:T(8,128)(2,1)S(1)}, bf16[192,512]{1,0:T(8,128)(2,1)S(1)}, u32[]{:S(2)}, u32[]{:S(2)}) collective-permute-start(bf16[192,512]{1,0:T(8,128)(2,1)S(1)} %bitcast.129), channel_id=1, source_target_pairs={{0,16},{16,0},{4,20},{20,4},{8,24},{24,8},{12,28},{28,12},{1,17},{... | collective-permute-start | bytes 589832 | tf_op jit(solution)/shard_map/ppermute | solution.py:36
  47.0 1.1 %fusion.79 = f32[512,192]{0,1:T(8,128)S(1)} fusion(bf16[512,192]{0,1:T(8,128)(2,1)S(1)} %fusion.6, bf16[1,5,2,192,192]{4,3,2,1,0:T(8,128)(2,1)} %param.12), kind=kOutput, calls=%fused_computation.99 | convolution fusion | flops 37748736 | bytes 688128 | tf_op jit(solution)/shard_map/dot_general | solution.py:79
  48.1 4.1 %collective-permute-done.6 = bf16[192,512]{1,0:T(8,128)(2,1)S(1)} collective-permute-done((bf16[192,512]{1,0:T(8,128)(2,1)S(1)}, bf16[192,512]{1,0:T(8,128)(2,1)S(1)}, u32[]{:S(2)}, u32[]{:S(2)}) %collective-permute-start.6) | collective-permute-done | bytes 196640 | tf_op jit(solution)/shard_map/ppermute | solution.py:36
  52.3 1.0 %gather_fusion.2 = bf16[192,512]{1,0:T(8,128)(2,1)S(1)} fusion(bf16[192,512]{1,0:T(8,128)(2,1)S(1)} %collective-permute-done.6, s32[1024]{0:T(1024)S(1)} %pad_clamp_fusion.2), kind=kCustom, calls=%fused_computation.2 | custom fusion | bytes 393984 | tf_op jit(solution)/shard_map/gather | solution.py:78
  53.3 1.2 %fusion.7 = bf16[512,192]{0,1:T(8,128)(2,1)S(1)} fusion(f32[512,192]{0,1:T(8,128)S(1)} %fusion.79, bf16[192,512]{1,0:T(8,128)(2,1)S(1)} %gather_fusion.2, bf16[1,5,2,192,192]{4,3,2,1,0:T(8,128)(2,1)} %param.12), kind=kOutput, calls=%fused_computation.22 | convolution fusion | flops 37945344 | bytes 884736 | tf_op jit(solution)/shard_map/dot_general | solution.py:80
  54.5 1.1 %fusion.76 = f32[512,192]{0,1:T(8,128)S(1)} fusion(bf16[512,192]{0,1:T(8,128)(2,1)S(1)} %fusion.7, bf16[1,5,2,192,192]{4,3,2,1,0:T(8,128)(2,1)} %param.12), kind=kOutput, calls=%fused_computation.96 | convolution fusion | flops 37748736 | bytes 688128 | tf_op jit(solution)/shard_map/dot_general | solution.py:86
  55.6 8.4 %collective-permute-done.7 = bf16[192,512]{1,0:T(8,128)(2,1)S(1)} collective-permute-done((bf16[192,512]{1,0:T(8,128)(2,1)S(1)}, bf16[192,512]{1,0:T(8,128)(2,1)S(1)}, u32[]{:S(2)}, u32[]{:S(2)}) %collective-permute-start.7) | collective-permute-done | bytes 196640 | tf_op jit(solution)/shard_map/ppermute | solution.py:36
  64.0 1.0 %gather_fusion.3 = bf16[192,512]{1,0:T(8,128)(2,1)S(1)} fusion(bf16[192,512]{1,0:T(8,128)(2,1)S(1)} %collective-permute-done.7, s32[1024]{0:T(1024)S(1)} %pad_clamp_fusion.1), kind=kCustom, calls=%fused_computation.3 | custom fusion | bytes 393984 | tf_op jit(solution)/shard_map/gather | solution.py:85
  65.0 1.1 %fusion.8 = bf16[512,192]{0,1:T(8,128)(2,1)S(1)} fusion(f32[512,192]{0,1:T(8,128)S(1)} %fusion.76, bf16[192,512]{1,0:T(8,128)(2,1)S(1)} %gather_fusion.3, bf16[1,5,2,192,192]{4,3,2,1,0:T(8,128)(2,1)} %param.12), kind=kOutput, calls=%fused_computation.23 | convolution fusion | flops 37945344 | bytes 884736 | tf_op jit(solution)/shard_map/dot_general | solution.py:89
  66.1 1.1 %collective-permute-start.8 = (bf16[192,512]{1,0:T(8,128)(2,1)S(1)}, bf16[192,512]{1,0:T(8,128)(2,1)S(1)}, u32[]{:S(2)}, u32[]{:S(2)}) collective-permute-start(bf16[192,512]{1,0:T(8,128)(2,1)S(1)} %bitcast.131), channel_id=1, source_target_pairs={{0,2},{2,0},{1,3},{3,1},{4,6},{6,4},{5,7},{7,5},{8,10},{10,8},{9,1... | collective-permute-start | bytes 589832 | tf_op jit(solution)/shard_map/ppermute | solution.py:36
  67.2 1.1 %fusion.73 = f32[512,192]{0,1:T(8,128)S(1)} fusion(bf16[512,192]{0,1:T(8,128)(2,1)S(1)} %fusion.8, bf16[1,5,2,192,192]{4,3,2,1,0:T(8,128)(2,1)} %param.12), kind=kOutput, calls=%fused_computation.93 | convolution fusion | flops 37748736 | bytes 688128 | tf_op jit(solution)/shard_map/dot_general | solution.py:86
  68.3 8.8 %collective-permute-done.8 = bf16[192,512]{1,0:T(8,128)(2,1)S(1)} collective-permute-done((bf16[192,512]{1,0:T(8,128)(2,1)S(1)}, bf16[192,512]{1,0:T(8,128)(2,1)S(1)}, u32[]{:S(2)}, u32[]{:S(2)}) %collective-permute-start.8) | collective-permute-done | bytes 196640 | tf_op jit(solution)/shard_map/ppermute | solution.py:36
  77.1 1.0 %gather_fusion.4 = bf16[192,512]{1,0:T(8,128)(2,1)S(1)} fusion(bf16[192,512]{1,0:T(8,128)(2,1)S(1)} %collective-permute-done.8, s32[1024]{0:T(1024)S(1)} %pad_clamp_fusion), kind=kCustom, calls=%fused_computation.4 | custom fusion | bytes 393984 | tf_op jit(solution)/shard_map/gather | solution.py:85
  78.1 1.4 %pad_maximum_fusion = bf16[6,512,512]{2,1,0:T(8,128)(2,1)S(1)} fusion(bf16[2,512,512]{2,1,0:T(8,128)(2,1)} %collective-permute-done.3, bf16[2,512,512]{2,1,0:T(8,128)(2,1)S(1)} %bitcast.127, bf16[2,512,512]{2,1,0:T(8,128)(2,1)S(1)} %collective-permute-done.2), kind=kLoop, calls=%fused_computation.5 | loop fusion | flops 3145728 | bytes 6291456 | tf_op jit(solution)/shard_map/concatenate | solution.py:25
  83.0 2.5 %fusion = bf16[2,512,512]{2,1,0:T(8,128)(2,1)} fusion(f32[1,512,512]{2,1,0:T(8,128)S(1)} %fusion.2, f32[1,512,512]{2,1,0:T(8,128)S(1)} %fusion.4, bf16[2,512,192]{1,2,0:T(8,128)(2,1)S(1)} %copy-done, f32[512,192]{0,1:T(8,128)S(1)} %fusion.73, bf16[192,512]{1,0:T(8,128)(2,1)S(1)} %gather_fusion.4, bf16[1,5,2,192,192]{4,3,2,1,0:T(8,128)(2,1)} %param.12), kind=kOutput, calls=%fused_computation.7 | convolution fusion | flops 240844800 | bytes 4227072 | tf_op jit(solution)/shard_map/nlr,rc->nlc/dot_general | solution.py:93
  (31 shorter events, 3.7 us)
Async XLA Ops:
  0.0 83.0 %copy-start = (bf16[2,512,192]{1,2,0:T(8,128)(2,1)S(1)}, bf16[2,512,192]{1,2,0:T(8,128)(2,1)}, u32[]{:S(2)}) copy-start(bf16[2,512,192]{1,2,0:T(8,128)(2,1)} %param.11) | copy-start | bytes 1179652
  0.0 30.9 %copy-start.2 = (bf16[2,2,512]{2,1,0:T(2,128)(2,1)S(1)}, bf16[2,2,512]{2,1,0:T(2,128)(2,1)}, u32[]{:S(2)}) copy-start(bf16[2,2,512]{2,1,0:T(2,128)(2,1)} %param.8) | copy-start | bytes 12292
  0.0 30.8 %collective-permute-start = (bf16[2,2,512]{2,1,0:T(2,128)(2,1)}, bf16[2,2,512]{2,1,0:T(2,128)(2,1)S(1)}, u32[]{:S(2)}, u32[]{:S(2)}) collective-permute-start(bf16[2,2,512]{2,1,0:T(2,128)(2,1)} %param.8), channel_id=1, source_target_pairs={{0,1},{1,2},{2,3},{3,4},{4,5},{5,6},{6,7},{7,8},{8,9},{9,10},{10,1... | collective-permute-start | bytes 12296 | tf_op jit(solution)/shard_map/ppermute | solution.py:23
  4.2 26.7 %collective-permute-start.1 = (bf16[2,2,512]{2,1,0:T(2,128)(2,1)}, bf16[2,2,512]{2,1,0:T(2,128)(2,1)S(1)}, u32[]{:S(2)}, u32[]{:S(2)}) collective-permute-start(bf16[2,2,512]{2,1,0:T(2,128)(2,1)} %param.8), channel_id=1, source_target_pairs={{1,0},{2,1},{3,2},{4,3},{5,4},{6,5},{7,6},{8,7},{9,8},{10,9},{11,1... | collective-permute-start | bytes 12296 | tf_op jit(solution)/shard_map/ppermute | solution.py:24
  8.7 69.4 %collective-permute-start.2 = (bf16[2,512,512]{2,1,0:T(8,128)(2,1)}, bf16[2,512,512]{2,1,0:T(8,128)(2,1)S(1)}, u32[]{:S(2)}, u32[]{:S(2)}) collective-permute-start(bf16[2,512,512]{2,1,0:T(8,128)(2,1)} %bitcast.125), channel_id=1, source_target_pairs={{0,1},{1,2},{2,3},{3,4},{4,5},{5,6},{6,7},{7,8},{8,9},{9,10},{10,1... | collective-permute-start | bytes 3145736 | tf_op jit(solution)/shard_map/ppermute | solution.py:23
  10.6 67.5 %collective-permute-start.3 = (bf16[2,512,512]{2,1,0:T(8,128)(2,1)}, bf16[2,512,512]{2,1,0:T(8,128)(2,1)}, u32[]{:S(2)}, u32[]{:S(2)}) collective-permute-start(bf16[2,512,512]{2,1,0:T(8,128)(2,1)} %bitcast.126), channel_id=1, source_target_pairs={{1,0},{2,1},{3,2},{4,3},{5,4},{6,5},{7,6},{8,7},{9,8},{10,9},{11,1... | collective-permute-start | bytes 3145736 | tf_op jit(solution)/shard_map/ppermute | solution.py:24
  18.9 12.1 %collective-permute-start.4 = (bf16[192,512]{1,0:T(8,128)(2,1)S(1)}, bf16[192,512]{1,0:T(8,128)(2,1)S(1)}, u32[]{:S(2)}, u32[]{:S(2)}) collective-permute-start(bf16[192,512]{1,0:T(8,128)(2,1)S(1)} %fusion.10), channel_id=1, source_target_pairs={{0,4},{4,0},{8,12},{12,8},{16,20},{20,16},{24,28},{28,24},{1,5},{5... | collective-permute-start | bytes 589832 | tf_op jit(solution)/shard_map/ppermute | solution.py:36
  33.1 10.8 %collective-permute-start.5 = (bf16[192,512]{1,0:T(8,128)(2,1)S(1)}, bf16[192,512]{1,0:T(8,128)(2,1)S(1)}, u32[]{:S(2)}, u32[]{:S(2)}) collective-permute-start(bf16[192,512]{1,0:T(8,128)(2,1)S(1)} %bitcast.128), channel_id=1, source_target_pairs={{0,8},{8,0},{4,12},{12,4},{16,24},{24,16},{20,28},{28,20},{1,9},{9... | collective-permute-start | bytes 589832 | tf_op jit(solution)/shard_map/ppermute | solution.py:36
  46.0 6.2 %collective-permute-start.6 = (bf16[192,512]{1,0:T(8,128)(2,1)S(1)}, bf16[192,512]{1,0:T(8,128)(2,1)S(1)}, u32[]{:S(2)}, u32[]{:S(2)}) collective-permute-start(bf16[192,512]{1,0:T(8,128)(2,1)S(1)} %bitcast.129), channel_id=1, source_target_pairs={{0,16},{16,0},{4,20},{20,4},{8,24},{24,8},{12,28},{28,12},{1,17},{... | collective-permute-start | bytes 589832 | tf_op jit(solution)/shard_map/ppermute | solution.py:36
  53.3 24.9 %copy-start.1 = (bf16[1024,512]{1,0:T(8,128)(2,1)S(1)}, bf16[1024,512]{1,0:T(8,128)(2,1)}, u32[]{:S(2)}) copy-start(bf16[1024,512]{1,0:T(8,128)(2,1)} %param.7) | copy-start | bytes 3145732
  54.5 9.6 %collective-permute-start.7 = (bf16[192,512]{1,0:T(8,128)(2,1)S(1)}, bf16[192,512]{1,0:T(8,128)(2,1)S(1)}, u32[]{:S(2)}, u32[]{:S(2)}) collective-permute-start(bf16[192,512]{1,0:T(8,128)(2,1)S(1)} %bitcast.130), channel_id=1, source_target_pairs={{0,1},{1,0},{2,3},{3,2},{4,5},{5,4},{6,7},{7,6},{8,9},{9,8},{10,11... | collective-permute-start | bytes 589832 | tf_op jit(solution)/shard_map/ppermute | solution.py:36
  66.1 11.0 %collective-permute-start.8 = (bf16[192,512]{1,0:T(8,128)(2,1)S(1)}, bf16[192,512]{1,0:T(8,128)(2,1)S(1)}, u32[]{:S(2)}, u32[]{:S(2)}) collective-permute-start(bf16[192,512]{1,0:T(8,128)(2,1)S(1)} %bitcast.131), channel_id=1, source_target_pairs={{0,2},{2,0},{1,3},{3,1},{4,6},{6,4},{5,7},{7,5},{8,10},{10,8},{9,1... | collective-permute-start | bytes 589832 | tf_op jit(solution)/shard_map/ppermute | solution.py:36
where the time goes:
time: 86.7 us; the launch traced here: 85.5 us
  waiting for transfers between devices  27.7 us (32%)
  starting transfers between devices  21.7 us (25%)
  matrix products  18.6 us (21%)
  between operations  7.8 us (9%)
  local copies, waits for them, and re-layouts  7.41 us (9%)
  other arithmetic  2.38 us (3%)
    ppermute x5, waiting for transfers between devices, from_partner(): return lax.ppermute(block, axis, route)  27.7 us
    ppermute x2, starting transfers between devices, padded(): after = lax.ppermute(initial, axis, down)  9.95 us
    ppermute x2, starting transfers between devices, padded(): before = lax.ppermute(last, axis, up)  6.07 us
    ppermute x5, starting transfers between devices, from_partner(): return lax.ppermute(block, axis, route)  5.65 us
    dot_general x6, matrix products, on_device(): jnp.dot(tile, source_rows, preferred_element_type=jnp.float32)  3.41 us
    dot_general x3, matrix products, on_device(): jnp.dot(transfer[0, level_bit, 1], partner_rows, preferred_element_type=j...  3.38 us
    dot_general x3, matrix products, on_device(): jnp.dot(transfer[0, level_bit, 0], projected, preferred_element_type=jnp....  3.25 us
    gather x3, local copies, waits for them, and re-layouts, on_device(): from_partner(projected, 'wide', level_bit)[level_perm[level_bit]]  3 us
  transfers between devices with their start and end apart: 9, of which 4 were waited for; matrix products, arithmetic and copies ran while one was open for 25% of the time, Pallas kernels for 0%

commit v1 on v0

v1 whole, which is shorter than its diff:
```python
import functools
import math

import jax
import jax.numpy as jnp
from jax import lax
from jax.experimental import pallas as pl
from jax.experimental.pallas import tpu as pltpu
from jax.sharding import PartitionSpec as P

NB = 3
LW = 3
SOFTENING = 0.0004
MESH = pl.DeviceIdType.MESH
PIECES = 4
FIRST = 4
SECOND = 2


def kernel(
    sizes,
    near_ref,
    rhs_ref,
    coords_ref,
    project_ref,
    expand_ref,
    transfer_ref,
    perm_ref,
    out_ref,
    below_ref,
    above_ref,
    below_raw,
    above_raw,
    points,
    targets,
    total,
    state,
    partner_state,
    partner_transfer,
    up_send,
    down_send,
    below_recv,
    above_recv,
    point_send,
    point_recv,
    level_send,
    level_recv,
):
    wide_count, pair_count = sizes
    leaves, _, leaf_rows = coords_ref.shape
    levels, rank = perm_ref.shape
    piece = leaf_rows // PIECES
    wide, pair = lax.axis_index("wide"), lax.axis_index("pair")
    count = wide_count * pair_count
    me = wide * pair_count + pair
    not_first = me > 0
    not_last = me < count - 1

    def place(device):
        return (lax.div(device, pair_count), lax.rem(device, pair_count))

    up = place(lax.rem(me + 1, count))
    down = place(lax.rem(me + count - 1, count))

    def partner(level):
        if level < LW:
            bit = 1 << level
            digit = lax.rem(lax.div(wide, bit), 2)
            return (wide + bit - 2 * bit * digit, pair)
        bit = 1 << (level - LW)
        digit = lax.rem(lax.div(pair, bit), 2)
        return (wide, pair + bit - 2 * bit * digit)

    barrier = pltpu.get_barrier_semaphore()
    peers = [up, down] + [partner(level) for level in range(levels)]
    for peer in peers:
        pl.semaphore_signal(barrier, inc=1, device_id=peer, device_id_type=MESH)

    @pl.when(jnp.logical_not(not_first))
    def _():
        below_ref[...] = jnp.zeros_like(below_ref)
        below_raw[...] = jnp.zeros_like(below_raw)

    @pl.when(jnp.logical_not(not_last))
    def _():
        above_ref[...] = jnp.zeros_like(above_ref)
        above_raw[...] = jnp.zeros_like(above_raw)

    pl.semaphore_wait(barrier, len(peers))

    def rows_up(c):
        leaf = leaves - 1 - lax.div(c, PIECES)
        return pl.ds(pl.multiple_of(leaf * leaf_rows + lax.rem(c, PIECES) * piece, piece), piece)

    def rows_down(c):
        return pl.ds(pl.multiple_of(c * piece, piece), piece)

    def copy_up(c):
        return pltpu.make_async_remote_copy(
            src_ref=rhs_ref.at[rows_up(c)],
            dst_ref=below_ref.at[rows_up(c)],
            send_sem=up_send.at[c],
            recv_sem=below_recv.at[c],
            device_id=up,
            device_id_type=MESH,
        )

    def copy_down(c):
        return pltpu.make_async_remote_copy(
            src_ref=rhs_ref.at[rows_down(c)],
            dst_ref=above_ref.at[rows_down(c)],
            send_sem=down_send.at[c],
            recv_sem=above_recv.at[c],
            device_id=down,
            device_id_type=MESH,
        )

    def point_copy(way, target, destination):
        return pltpu.make_async_remote_copy(
            src_ref=coords_ref,
            dst_ref=destination,
            send_sem=point_send.at[way],
            recv_sem=point_recv.at[way],
            device_id=target,
            device_id_type=MESH,
        )

    points_up = point_copy(0, up, below_raw)
    points_down = point_copy(1, down, above_raw)

    def send_halo(low, high):
        @pl.loop(low, high)
        def _(c):
            @pl.when(not_first)
            def _():
                copy_down(c).start()

            @pl.when(not_last)
            def _():
                copy_up(c).start()

    def level_copy(level):
        return pltpu.make_async_remote_copy(
            src_ref=state.at[level],
            dst_ref=partner_state.at[level],
            send_sem=level_send.at[level],
            recv_sem=level_recv.at[level],
            device_id=partner(level),
            device_id_type=MESH,
        )

    @pl.when(not_last)
    def _():
        points_up.start()

    @pl.when(not_first)
    def _():
        points_down.start()

    send_halo(0, FIRST)

    def dot(a, b, contract=(1, 0)):
        return lax.dot_general(
            a, b, (((contract[0],), (contract[1],)), ((), ())), preferred_element_type=jnp.float32
        )

    projected = sum(
        dot(project_ref[leaf], rhs_ref[leaf * leaf_rows : (leaf + 1) * leaf_rows])
        for leaf in range(leaves)
    )
    state[0] = projected.astype(jnp.bfloat16)
    level_copy(0).start()

    rank_rows = lax.broadcasted_iota(jnp.int32, (rank, rank), 0)
    for level in range(levels):
        chosen = jnp.where(rank_rows == perm_ref[level : level + 1, :], 1.0, 0.0)
        partner_transfer[level] = dot(
            transfer_ref[0, level, 1], chosen.astype(jnp.bfloat16), (1, 1)
        ).astype(jnp.bfloat16)

    for leaf in range(leaves):
        own = coords_ref[leaf].astype(jnp.float32)
        points[leaf + leaves] = own
        for axis in range(2):
            targets[leaf, axis] = jnp.broadcast_to(own[axis : axis + 1, :], (piece, leaf_rows)).T
    total[...] = jnp.zeros_like(total)

    factor = 0.25 / math.sqrt(leaf_rows)

    def scale(target, offset):
        inside = (me * leaves + target + offset >= 0) & (me * leaves + target + offset < count * leaves)
        found = near_ref[target, 0] == offset
        for slot in range(1, NB):
            found = found | (near_ref[target, slot] == offset)
        return jnp.where(found & inside, jnp.float32(factor), jnp.float32(0.0))

    def tile(target, source, c):
        columns = pl.ds(pl.multiple_of(c * piece, piece), piece)
        x = points[source + leaves, 0:1, columns]
        y = points[source + leaves, 1:2, columns]
        dx = targets[target, 0] - x
        dy = targets[target, 1] - y
        value = lax.rsqrt(dx * dx + dy * dy + SOFTENING) * scale(target, source - target)
        return value.astype(jnp.bfloat16)

    def rows_of(source, c):
        leaf = source % leaves
        rows = pl.ds(pl.multiple_of(leaf * leaf_rows + c * piece, piece), piece)
        ref = rhs_ref if 0 <= source < leaves else (below_ref if source < 0 else above_ref)
        return ref[rows, :]

    def near(target, sources, c):
        tiles = jnp.concatenate([tile(target, source, c) for source in sources], axis=1)
        block = jnp.concatenate([rows_of(source, c) for source in sources], axis=0)
        total[target] += dot(tiles, block)

    def near_own(low, high):
        @pl.loop(low, high)
        def _(c):
            for target in range(leaves):
                near(target, list(range(leaves)), c)

    done = 0
    for level in range(levels):
        own_part = dot(transfer_ref[0, level, 0], state[level])
        if done < PIECES:
            near_own(done, done + 1)
            done += 1
        level_copy(level).wait_recv()
        state[level + 1] = (
            own_part + dot(partner_transfer[level], partner_state[level])
        ).astype(jnp.bfloat16)
        if level + 1 < levels:
            level_copy(level + 1).start()
        if level + 1 == LW:
            send_halo(FIRST, FIRST + SECOND)
        if level + 1 == LW + 1:
            send_halo(FIRST + SECOND, leaves * PIECES)
    for leaf in range(leaves):
        total[leaf] += dot(expand_ref[leaf], state[levels], (0, 0))

    @pl.when(not_first)
    def _():
        points_up.wait_recv()

    @pl.when(not_last)
    def _():
        points_down.wait_recv()

    for leaf in range(leaves):
        points[leaf] = below_raw[leaf].astype(jnp.float32)
        points[leaf + 2 * leaves] = above_raw[leaf].astype(jnp.float32)

    for phase in range(leaves):
        low, high = -1 - phase, leaves + phase

        @pl.loop(0, PIECES)
        def _(c):
            at = phase * PIECES + c

            @pl.when(not_first)
            def _():
                copy_up(at).wait_recv()

            @pl.when(not_last)
            def _():
                copy_down(at).wait_recv()

            for target in range(leaves):
                sources = [s for s in (low, high) if abs(s - target) <= leaves]
                near(target, sources, c)

    out_ref[...] = total[...].astype(out_ref.dtype)

    for level in range(levels):
        level_copy(level).wait_send()

    @pl.when(not_last)
    def _():
        points_up.wait_send()

        @pl.loop(0, leaves * PIECES)
        def _(c):
            copy_up(c).wait_send()

    @pl.when(not_first)
    def _():
        points_down.wait_send()

        @pl.loop(0, leaves * PIECES)
        def _(c):
            copy_down(c).wait_send()


def on_device(sizes, rhs, coords, near_index, project_basis, expand_basis, transfer, level_perm):
    leaves, _, leaf_rows = coords.shape
    rows, columns = rhs.shape
    levels, rank = level_perm.shape
    pieces = leaves * PIECES
    dma = pltpu.SemaphoreType.DMA
    vmem = pl.BlockSpec(memory_space=pltpu.VMEM)
    smem = pl.BlockSpec(memory_space=pltpu.SMEM)
    out = pl.pallas_call(
        functools.partial(kernel, sizes),
        out_shape=jax.ShapeDtypeStruct((leaves, leaf_rows, columns), jnp.bfloat16),
        in_specs=[smem] + [vmem] * 6,
        out_specs=vmem,
        scratch_shapes=[
            pltpu.VMEM((rows, columns), jnp.bfloat16),
            pltpu.VMEM((rows, columns), jnp.bfloat16),
            pltpu.VMEM(coords.shape, coords.dtype),
            pltpu.VMEM(coords.shape, coords.dtype),
            pltpu.VMEM((3 * leaves, 2, leaf_rows), jnp.float32),
            pltpu.VMEM((leaves, 2, leaf_rows, leaf_rows // PIECES), jnp.float32),
            pltpu.VMEM((leaves, leaf_rows, columns), jnp.float32),
            pltpu.VMEM((levels + 1, rank, columns), jnp.bfloat16),
            pltpu.VMEM((levels, rank, columns), jnp.bfloat16),
            pltpu.VMEM((levels, rank, rank), jnp.bfloat16),
            dma((pieces,)),
            dma((pieces,)),
            dma((pieces,)),
            dma((pieces,)),
            dma((2,)),
            dma((2,)),
            dma((levels,)),
            dma((levels,)),
        ],
        compiler_params=pltpu.CompilerParams(
            collective_id=0, has_side_effects=True, vmem_limit_bytes=48 * 1024 * 1024
        ),
        name="operator",
    )(
        near_index,
        rhs,
        coords,
        project_basis.swapaxes(1, 2),
        expand_basis.swapaxes(1, 2),
        transfer,
        level_perm,
    )
    return out.reshape(rows, columns)


def solution(mesh):
    sizes = (mesh.shape["wide"], mesh.shape["pair"])
    return jax.shard_map(
        functools.partial(on_device, sizes),
        mesh=mesh,
        in_specs=(
            P(("wide", "pair"), None),
            P(("wide", "pair"), None, None),
            P(("wide", "pair"), None),
            P(("wide", "pair"), None, None),
            P(("wide", "pair"), None, None),
            P(("wide", "pair"), None, None, None, None),
            P(),
        ),
        out_specs=P(("wide", "pair"), None),
        check_vma=False,
    )
```

time: 86.7 us -> 69.6 us (0.80)
  Pallas kernels: 0 us -> 61.7 us
  waiting for transfers between devices: 27.7 us -> 0 us
  starting transfers between devices: 21.7 us -> 0 us
  matrix products: 18.6 us -> 0 us
  between operations: 7.8 us -> 0.02 us
  other arithmetic: 2.38 us -> 0 us
    pallas_call x0 -> x1, Pallas kernels: none -> 61.7 us  [on_device(): pl.pallas_call(functools.partial(kernel, sizes), out_shape=jax.ShapeDtype...]
    ppermute x9 -> x0, waiting for transfers between devices: 27.7 us -> none  [the longest x5 27.7 us: from_partner(): return lax.ppermute(block, axis, route)]
    ppermute x9 -> x0, starting transfers between devices: 21.7 us -> none  [the longest x2 9.95 us: padded(): after = lax.ppermute(initial, axis, down)]
    dot_general x18 -> x0, matrix products: 18.6 us -> none  [the longest x6 3.41 us: on_device(): jnp.dot(tile, source_rows, preferred_element_type=jnp.float32)]
    unnamed x8 -> x15, local copies, waits for them, and re-layouts: 0.03 us -> 7.45 us
    gather x5 -> x0, local copies, waits for them, and re-layouts: 5.01 us -> none  [the longest x3 3 us: on_device(): from_partner(projected, 'wide', level_bit)[level_perm[level_bit]]]
    slice x5 -> x0, local copies, waits for them, and re-layouts: 2.35 us -> none  [the longest x1 1.56 us: on_device(): position = target + 2 + near_index[target, slot]]
    concatenate x1 -> x0, other arithmetic: 1.43 us -> none  [padded(): x = jnp.concatenate([before, x, after], axis=dim)]
  transfers between devices with their start and end apart: 9 -> 0, of which waited for: 4 -> 0; matrix products, arithmetic and copies ran while one was open for 25% -> 0% of each run, Pallas kernels for 0% -> 0%
where the time goes in v1:
time: 69.6 us; the launch traced here: 69.2 us
  Pallas kernels  61.7 us (89%)
  local copies, waits for them, and re-layouts  7.45 us (11%)
    pallas_call x1, Pallas kernels, on_device(): pl.pallas_call(functools.partial(kernel, sizes), out_shape=jax.ShapeDtype...  61.7 us
    unnamed x15, local copies, waits for them, and re-layouts  7.45 us

profile of v1, /device:TPU:1, one launch (start us, length us, event | category | flops | bytes accessed | tf_op | source)
XLA Modules:
  0.0 69.2 jit_solution(10203463880774195023)
XLA Ops:
  0.0 0.0 copy-start.6
  0.0 0.7 copy-done.6
  0.7 0.0 copy-start
  0.7 1.2 %copy-done = bf16[1024,512]{1,0:T(8,128)(2,1)S(1)} copy-done((bf16[1024,512]{1,0:T(8,128)(2,1)S(1)}, bf16[1024,512]{1,0:T(8,128)(2,1)}, u32[]{:S(2)}) %copy-start) | copy-done | bytes 1048600
  1.9 0.0 copy-start.1
  1.9 1.2 %copy-done.1 = bf16[1,5,2,192,192]{4,3,2,1,0:T(8,128)(2,1)S(1)} copy-done((bf16[1,5,2,192,192]{4,3,2,1,0:T(8,128)(2,1)S(1)}, bf16[1,5,2,192,192]{4,3,2,1,0:T(8,128)(2,1)}, u32[]{:S(2)}) %copy-start.1) | copy-done | bytes 737304
  3.1 0.0 copy-start.2
  3.1 1.0 %copy-done.2 = bf16[2,512,192]{1,2,0:T(8,128)(2,1)S(1)} copy-done((bf16[2,512,192]{1,2,0:T(8,128)(2,1)S(1)}, bf16[2,512,192]{1,2,0:T(8,128)(2,1)}, u32[]{:S(2)}) %copy-start.2) | copy-done | bytes 393240
  4.1 0.0 copy-start.3
  4.1 1.0 %copy-done.3 = bf16[2,512,192]{1,2,0:T(8,128)(2,1)S(1)} copy-done((bf16[2,512,192]{1,2,0:T(8,128)(2,1)S(1)}, bf16[2,512,192]{1,2,0:T(8,128)(2,1)}, u32[]{:S(2)}) %copy-start.3) | copy-done | bytes 393240
  5.1 0.0 copy-start.4
  5.1 0.7 %copy-done.4 = s32[5,192]{1,0:T(8,128)S(1)} copy-done((s32[5,192]{1,0:T(8,128)S(1)}, s32[5,192]{1,0:T(8,128)}, u32[]{:S(2)}) %copy-start.4) | copy-done | bytes 3864
  5.8 0.0 copy-start.5
  5.8 0.7 copy-done.5
  6.5 61.7 %operator.1 = bf16[2,512,512]{2,1,0:T(8,128)(2,1)S(1)} custom-call(s32[2,3]{1,0:T(2,128)S(1)} %copy-done.6, bf16[1024,512]{1,0:T(8,128)(2,1)S(1)} %copy-done, bf16[2,2,512]{2,1,0:T(2,128)(2,1)S(1)} %copy-done.5, bf16[2,192,512]{2,1,0:T(8,128)(2,1)S(1)} %bitcast.4, bf16[2,192,512]{2,1,0:T(8,128)(2,1)S(1)} %bitcast.5, ...), custom_call_target="tpu_custom_call" | custom-call | tf_op jit(solution)/shard_map/operator/pallas_call | solution.py:303
  68.2 1.0 %copy.9 = bf16[1024,512]{1,0:T(8,128)(2,1)} copy(bf16[1024,512]{1,0:T(8,128)(2,1)S(1)} %bitcast.3) | data formatting | bytes 2097152
Async XLA Ops:
  0.0 0.7 copy-start.6
  0.7 1.2 %copy-start = (bf16[1024,512]{1,0:T(8,128)(2,1)S(1)}, bf16[1024,512]{1,0:T(8,128)(2,1)}, u32[]{:S(2)}) copy-start(bf16[1024,512]{1,0:T(8,128)(2,1)} %rhs_ref.1) | copy-start | bytes 3145732
  1.9 1.2 %copy-start.1 = (bf16[1,5,2,192,192]{4,3,2,1,0:T(8,128)(2,1)S(1)}, bf16[1,5,2,192,192]{4,3,2,1,0:T(8,128)(2,1)}, u32[]{:S(2)}) copy-start(bf16[1,5,2,192,192]{4,3,2,1,0:T(8,128)(2,1)} %transfer_ref.1) | copy-start | bytes 2211844
  3.1 1.0 %copy-start.2 = (bf16[2,512,192]{1,2,0:T(8,128)(2,1)S(1)}, bf16[2,512,192]{1,2,0:T(8,128)(2,1)}, u32[]{:S(2)}) copy-start(bf16[2,512,192]{1,2,0:T(8,128)(2,1)} %param.10) | copy-start | bytes 1179652
  4.1 1.0 %copy-start.3 = (bf16[2,512,192]{1,2,0:T(8,128)(2,1)S(1)}, bf16[2,512,192]{1,2,0:T(8,128)(2,1)}, u32[]{:S(2)}) copy-start(bf16[2,512,192]{1,2,0:T(8,128)(2,1)} %param.11) | copy-start | bytes 1179652
  5.1 0.7 %copy-start.4 = (s32[5,192]{1,0:T(8,128)S(1)}, s32[5,192]{1,0:T(8,128)}, u32[]{:S(2)}) copy-start(s32[5,192]{1,0:T(8,128)} %perm_ref.1) | copy-start | bytes 11524
  5.8 0.7 copy-start.5

commit v2 on v1

--- a/solution.py
+++ b/solution.py
@@ -13,12 +13,21 @@
 SOFTENING = 0.0004
 MESH = pl.DeviceIdType.MESH
 PIECES = 4
-FIRST = 4
+VMEM_GRANT = 65000000
+FIRST = 3
 SECOND = 2
 
 
 def kernel(
     sizes,
+    near_hbm,
+    rhs_hbm,
+    coords_hbm,
+    project_hbm,
+    expand_hbm,
+    transfer_hbm,
+    perm_hbm,
+    out_ref,
     near_ref,
     rhs_ref,
     coords_ref,
@@ -26,7 +35,7 @@
     expand_ref,
     transfer_ref,
     perm_ref,
-    out_ref,
+    load_sem,
     below_ref,
     above_ref,
     below_raw,
@@ -71,10 +80,26 @@
         digit = lax.rem(lax.div(pair, bit), 2)
         return (wide, pair + bit - 2 * bit * digit)
 
+    loads = [
+        pltpu.make_async_copy(source, destination, load_sem.at[i])
+        for i, (source, destination) in enumerate(
+            (
+                (project_hbm, project_ref),
+                (rhs_hbm, rhs_ref),
+                (perm_hbm, perm_ref),
+                (transfer_hbm, transfer_ref),
+                (coords_hbm, coords_ref),
+                (near_hbm, near_ref),
+                (expand_hbm, expand_ref),
+            )
+        )
+    ]
     barrier = pltpu.get_barrier_semaphore()
     peers = [up, down] + [partner(level) for level in range(levels)]
     for peer in peers:
         pl.semaphore_signal(barrier, inc=1, device_id=peer, device_id_type=MESH)
+    for load in loads:
+        load.start()
 
     @pl.when(jnp.logical_not(not_first))
     def _():
@@ -97,7 +122,7 @@
 
     def copy_up(c):
         return pltpu.make_async_remote_copy(
-            src_ref=rhs_ref.at[rows_up(c)],
+            src_ref=rhs_hbm.at[rows_up(c)],
             dst_ref=below_ref.at[rows_up(c)],
             send_sem=up_send.at[c],
             recv_sem=below_recv.at[c],
@@ -107,7 +132,7 @@
 
     def copy_down(c):
         return pltpu.make_async_remote_copy(
-            src_ref=rhs_ref.at[rows_down(c)],
+            src_ref=rhs_hbm.at[rows_down(c)],
             dst_ref=above_ref.at[rows_down(c)],
             send_sem=down_send.at[c],
             recv_sem=above_recv.at[c],
@@ -117,7 +142,7 @@
 
     def point_copy(way, target, destination):
         return pltpu.make_async_remote_copy(
-            src_ref=coords_ref,
+            src_ref=coords_hbm,
             dst_ref=destination,
             send_sem=point_send.at[way],
             recv_sem=point_recv.at[way],
@@ -164,6 +189,8 @@
             a, b, (((contract[0],), (contract[1],)), ((), ())), preferred_element_type=jnp.float32
         )
 
+    loads[0].wait()
+    loads[1].wait()
     projected = sum(
         dot(project_ref[leaf], rhs_ref[leaf * leaf_rows : (leaf + 1) * leaf_rows])
         for leaf in range(leaves)
@@ -171,6 +198,8 @@
     state[0] = projected.astype(jnp.bfloat16)
     level_copy(0).start()
 
+    loads[2].wait()
+    loads[3].wait()
     rank_rows = lax.broadcasted_iota(jnp.int32, (rank, rank), 0)
     for level in range(levels):
         chosen = jnp.where(rank_rows == perm_ref[level : level + 1, :], 1.0, 0.0)
@@ -178,6 +207,8 @@
             transfer_ref[0, level, 1], chosen.astype(jnp.bfloat16), (1, 1)
         ).astype(jnp.bfloat16)
 
+    loads[4].wait()
+    loads[5].wait()
     for leaf in range(leaves):
         own = coords_ref[leaf].astype(jnp.float32)
         points[leaf + leaves] = own
@@ -236,6 +267,7 @@
             send_halo(FIRST, FIRST + SECOND)
         if level + 1 == LW + 1:
             send_halo(FIRST + SECOND, leaves * PIECES)
+    loads[6].wait()
     for leaf in range(leaves):
         total[leaf] += dot(expand_ref[leaf], state[levels], (0, 0))
 
@@ -299,13 +331,25 @@
     pieces = leaves * PIECES
     dma = pltpu.SemaphoreType.DMA
     vmem = pl.BlockSpec(memory_space=pltpu.VMEM)
-    smem = pl.BlockSpec(memory_space=pltpu.SMEM)
+    hbm = pl.BlockSpec(memory_space=pltpu.HBM)
+    operands = (
+        near_index,
+        rhs,
+        coords,
+        project_basis.swapaxes(1, 2),
+        expand_basis.swapaxes(1, 2),
+        transfer,
+        level_perm,
+    )
     out = pl.pallas_call(
         functools.partial(kernel, sizes),
-        out_shape=jax.ShapeDtypeStruct((leaves, leaf_rows, columns), jnp.bfloat16),
-        in_specs=[smem] + [vmem] * 6,
+        out_shape=pltpu.VMEM((leaves, leaf_rows, columns), jnp.bfloat16),
+        in_specs=[hbm] * len(operands),
         out_specs=vmem,
-        scratch_shapes=[
+        scratch_shapes=[pltpu.SMEM(near_index.shape, near_index.dtype)]
+        + [pltpu.VMEM(operand.shape, operand.dtype) for operand in operands[1:]]
+        + [
+            dma((len(operands),)),
             pltpu.VMEM((rows, columns), jnp.bfloat16),
             pltpu.VMEM((rows, columns), jnp.bfloat16),
             pltpu.VMEM(coords.shape, coords.dtype),
@@ -326,18 +370,10 @@
             dma((levels,)),
         ],
         compiler_params=pltpu.CompilerParams(
-            collective_id=0, has_side_effects=True, vmem_limit_bytes=48 * 1024 * 1024
+            collective_id=0, has_side_effects=True, vmem_limit_bytes=VMEM_GRANT
         ),
         name="operator",
-    )(
-        near_index,
-        rhs,
-        coords,
-        project_basis.swapaxes(1, 2),
-        expand_basis.swapaxes(1, 2),
-        transfer,
-        level_perm,
-    )
+    )(*operands)
     return out.reshape(rows, columns)
 
 

time: 69.6 us -> 62.7 us (0.901)
  local copies, waits for them, and re-layouts: 7.45 us -> 0.97 us
    unnamed x15 -> x1, local copies, waits for them, and re-layouts: 7.45 us -> 0.97 us
where the time goes in v2:
time: 62.7 us; the launch traced here: 62.6 us
  Pallas kernels  61.6 us (98%)
  local copies, waits for them, and re-layouts  0.97 us (2%)
    pallas_call x1, Pallas kernels, on_device(): pl.pallas_call(functools.partial(kernel, sizes), out_shape=pltpu.VMEM((le...  61.6 us

profile of v2, /device:TPU:1, one launch (start us, length us, event | category | flops | bytes accessed | tf_op | source)
XLA Modules:
  0.0 62.6 jit_solution(3516192267046697620)
XLA Ops:
  0.0 61.6 %operator.1 = bf16[2,512,512]{2,1,0:T(8,128)(2,1)S(1)} custom-call(s32[2,3]{1,0:T(2,128)} %near_hbm.1, bf16[1024,512]{1,0:T(8,128)(2,1)} %rhs_hbm.1, bf16[2,2,512]{2,1,0:T(2,128)(2,1)} %coords_hbm.1, bf16[2,192,512]{2,1,0:T(8,128)(2,1)} %bitcast.4, bf16[2,192,512]{2,1,0:T(8,128)(2,1)} %bitcast.5, bf16[1,5,2,192,192]{4,3,2,1,0:T(8,128)(2,1)} %transfer_hbm.1, ...), custom_call_target="tpu_custom_call" | custom-call | tf_op jit(solution)/shard_map/operator/pallas_call | solution.py:344
  61.6 1.0 %copy.9 = bf16[1024,512]{1,0:T(8,128)(2,1)} copy(bf16[1024,512]{1,0:T(8,128)(2,1)S(1)} %bitcast.3) | data formatting | bytes 2097152

commit v3 on v2

--- a/solution.py
+++ b/solution.py
@@ -14,7 +14,8 @@
 MESH = pl.DeviceIdType.MESH
 PIECES = 4
 VMEM_GRANT = 65000000
-FIRST = 3
+FIRST = 4
+MOVED = 2
 SECOND = 2
 
 
@@ -54,6 +55,9 @@
     point_recv,
     level_send,
     level_recv,
+    relay_ref,
+    relay_send,
+    relay_recv,
 ):
     wide_count, pair_count = sizes
     leaves, _, leaf_rows = coords_ref.shape
@@ -98,6 +102,28 @@
     peers = [up, down] + [partner(level) for level in range(levels)]
     for peer in peers:
         pl.semaphore_signal(barrier, inc=1, device_id=peer, device_id_type=MESH)
+    end = pair_count - 1
+    slots = wide_count // 2 - 1
+    far_up = (lax.rem(wide, 2) == 1) & (wide < wide_count - 1) & (pair == end)
+    far_down = (lax.rem(wide, 2) == 0) & (wide > 0) & (pair == 0)
+    relay_up = (wide >= wide_count - MOVED) & (pair == end)
+    relay_down = (wide < MOVED) & (pair == 0)
+
+    def greet(peer):
+        pl.semaphore_signal(barrier, inc=1, device_id=peer, device_id_type=MESH)
+
+    @pl.when(far_up | far_down)
+    def _():
+        for m in range(MOVED):
+            greet((wide_count - MOVED + m, end))
+            greet((m, 0))
+
+    @pl.when(relay_up | relay_down)
+    def _():
+        for slot in range(slots):
+            greet((2 * slot + 1, end))
+            greet((2 * slot + 2, 0))
+
     for load in loads:
         load.start()
 
@@ -111,7 +137,9 @@
         above_ref[...] = jnp.zeros_like(above_ref)
         above_raw[...] = jnp.zeros_like(above_raw)
 
-    pl.semaphore_wait(barrier, len(peers))
+    extra = jnp.where(far_up | far_down, 2 * MOVED, 0)
+    extra = extra + jnp.where(relay_up | relay_down, 2 * slots, 0)
+    pl.semaphore_wait(barrier, len(peers) + extra)
 
     def rows_up(c):
         leaf = leaves - 1 - lax.div(c, PIECES)
@@ -153,14 +181,58 @@
     points_up = point_copy(0, up, below_raw)
     points_down = point_copy(1, down, above_raw)
 
+    def to_relay(rows, send_sem, slot, relay):
+        return pltpu.make_async_remote_copy(
+            src_ref=rhs_hbm.at[rows],
+            dst_ref=relay_ref.at[slot],
+            send_sem=send_sem,
+            recv_sem=relay_recv.at[slot],
+            device_id=relay,
+            device_id_type=MESH,
+        )
+
+    def onward_up(slot):
+        c = wide - (wide_count - MOVED)
+        return pltpu.make_async_remote_copy(
+            src_ref=relay_ref.at[slot],
+            dst_ref=below_ref.at[rows_up(c)],
+            send_sem=relay_send.at[slot],
+            recv_sem=below_recv.at[c],
+            device_id=(2 * slot + 2, 0),
+            device_id_type=MESH,
+        )
+
+    def onward_down(slot):
+        return pltpu.make_async_remote_copy(
+            src_ref=relay_ref.at[slot],
+            dst_ref=above_ref.at[rows_down(wide)],
+            send_sem=relay_send.at[slot],
+            recv_sem=above_recv.at[wide],
+            device_id=(2 * slot + 1, end),
+            device_id_type=MESH,
+        )
+
     def send_halo(low, high):
         @pl.loop(low, high)
         def _(c):
-            @pl.when(not_first)
+            by_relay_down = far_down & (c < MOVED)
+            by_relay_up = far_up & (c < MOVED)
+
+            @pl.when(by_relay_down)
+            def _():
+                to_relay(rows_down(c), down_send.at[c], lax.div(wide, 2) - 1, (c, 0)).start()
+
+            @pl.when(not_first & jnp.logical_not(by_relay_down))
             def _():
                 copy_down(c).start()
 
-            @pl.when(not_last)
+            @pl.when(by_relay_up)
+            def _():
+                to_relay(
+                    rows_up(c), up_send.at[c], lax.div(wide, 2), (wide_count - MOVED + c, end)
+                ).start()
+
+            @pl.when(not_last & jnp.logical_not(by_relay_up))
             def _():
                 copy_up(c).start()
 
@@ -263,6 +335,20 @@
         ).astype(jnp.bfloat16)
         if level + 1 < levels:
             level_copy(level + 1).start()
+        if level == 0:
+
+            @pl.when(relay_up)
+            def _():
+                for slot in range(slots):
+                    to_relay(rows_down(0), relay_send.at[slot], slot, up).wait_recv()
+                    onward_up(slot).start()
+
+            @pl.when(relay_down)
+            def _():
+                for slot in range(slots):
+                    to_relay(rows_down(0), relay_send.at[slot], slot, up).wait_recv()
+                    onward_down(slot).start()
+
         if level + 1 == LW:
             send_halo(FIRST, FIRST + SECOND)
         if level + 1 == LW + 1:
@@ -307,6 +393,16 @@
     for level in range(levels):
         level_copy(level).wait_send()
 
+    @pl.when(relay_up)
+    def _():
+        for slot in range(slots):
+            onward_up(slot).wait_send()
+
+    @pl.when(relay_down)
+    def _():
+        for slot in range(slots):
+            onward_down(slot).wait_send()
+
     @pl.when(not_last)
     def _():
         points_up.wait_send()
@@ -329,6 +425,7 @@
     rows, columns = rhs.shape
     levels, rank = level_perm.shape
     pieces = leaves * PIECES
+    slots = sizes[0] // 2 - 1
     dma = pltpu.SemaphoreType.DMA
     vmem = pl.BlockSpec(memory_space=pltpu.VMEM)
     hbm = pl.BlockSpec(memory_space=pltpu.HBM)
@@ -368,6 +465,9 @@
             dma((2,)),
             dma((levels,)),
             dma((levels,)),
+            pltpu.VMEM((slots, leaf_rows // PIECES, columns), jnp.bfloat16),
+            dma((slots,)),
+            dma((slots,)),
         ],
         compiler_params=pltpu.CompilerParams(
             collective_id=0, has_side_effects=True, vmem_limit_bytes=VMEM_GRANT

time: 62.7 us -> 60.9 us (0.971)
  Pallas kernels: 61.6 us -> 59.7 us
    pallas_call x1, Pallas kernels: 61.6 us -> 59.7 us  [on_device(): pl.pallas_call(functools.partial(kernel, sizes), out_shape=pltpu.VMEM((le...]
where the time goes in v3:
time: 60.9 us; the launch traced here: 60.7 us
  Pallas kernels  59.7 us (98%)
  local copies, waits for them, and re-layouts  0.97 us (2%)
    pallas_call x1, Pallas kernels, on_device(): pl.pallas_call(functools.partial(kernel, sizes), out_shape=pltpu.VMEM((le...  59.7 us

profile of v3, /device:TPU:1, one launch (start us, length us, event | category | flops | bytes accessed | tf_op | source)
XLA Modules:
  0.0 60.7 jit_solution(4630290724462953875)
XLA Ops:
  0.0 59.7 %operator.1 = bf16[2,512,512]{2,1,0:T(8,128)(2,1)S(1)} custom-call(s32[2,3]{1,0:T(2,128)} %near_hbm.1, bf16[1024,512]{1,0:T(8,128)(2,1)} %rhs_hbm.1, bf16[2,2,512]{2,1,0:T(2,128)(2,1)} %coords_hbm.1, bf16[2,192,512]{2,1,0:T(8,128)(2,1)} %bitcast.4, bf16[2,192,512]{2,1,0:T(8,128)(2,1)} %bitcast.5, bf16[1,5,2,192,192]{4,3,2,1,0:T(8,128)(2,1)} %transfer_hbm.1, ...), custom_call_target="tpu_custom_call" | custom-call | tf_op jit(solution)/shard_map/operator/pallas_call | solution.py:441
  59.7 1.0 %copy.9 = bf16[1024,512]{1,0:T(8,128)(2,1)} copy(bf16[1024,512]{1,0:T(8,128)(2,1)S(1)} %bitcast.3) | data formatting | bytes 2097152
